TPU v7x, 32 devices: a whole 2x2x4 slice. The times are simulated.
32 devices in a mesh: dp: 4 (over y, x), vocab: 8 (over z, core).
Axes of the slice: x: 2, y: 2, z: 4, core: 2. Of those that a mesh axis runs over, the one named last changes fastest.
Arguments:
- hidden: bfloat16 [256, 3072], P(('dp', 'vocab')), parts along dimension 0, may hold values from -60 to 60
- weight: bfloat16 [3072, 8192], P(None, 'vocab'), may hold values from -0.32421875 to 0.32421875
- targets: int32 [256], P('dp'), parts along dimension 0, may hold values from 0 to 8191
Outputs:
- loss: float32 [4], P('dp'), parts along dimension 0
- d_hidden: bfloat16 [256, 3072], P(('dp', 'vocab')), parts along dimension 0
- d_weight: bfloat16 [12288, 8192], P('dp', 'vocab'), parts along dimension 0
There are 4 independent parts, one for each index of `dp`. A program takes and returns all parts, laid end to end along the dimension named above; an argument that names none is the same for every part. Nothing has to cross between parts.
All inputs are finite; a program needn't handle non-finite values.
Results may differ from a plain program's by a relative error of at most 0.0035.
Values may be sent and summed in bfloat16 or wider, within the bound.
A program may use at most 64 MiB of HBM per device.

v0:
```python
import jax
import jax.numpy as jnp
from jax import lax
from jax.sharding import PartitionSpec as P


def joined(value, axis, combine):
    everything = jax.tree.map(lambda part: lax.all_gather(part, axis), value)
    initial = jax.tree.map(lambda part: part[0], everything)

    def hop(k, so_far):
        return combine(so_far, jax.tree.map(lambda part: part[k], everything))

    return lax.fori_loop(1, lax.axis_size(axis), hop, initial)


def combine_stats(first, second):
    top = jnp.maximum(first[0], second[0])
    total = first[1] * jnp.exp(first[0] - top) + second[1] * jnp.exp(second[0] - top)
    return (top, total, first[2] + second[2])


def body(hidden, weight, targets):
    gathered = lax.all_gather(hidden, "vocab", axis=0, tiled=True)
    logits = jnp.dot(gathered, weight, preferred_element_type=jnp.float32)
    width = weight.shape[1]
    offset = lax.axis_index("vocab") * width
    columns = offset + lax.broadcasted_iota(jnp.int32, (1, width), 1)
    hits = columns == targets[:, None]
    picked_local = jnp.sum(jnp.where(hits, logits, jnp.zeros_like(logits)), axis=1)
    local_top = jnp.max(logits, axis=1)
    local_total = jnp.sum(jnp.exp(logits - local_top[:, None]), axis=1)
    top, total, picked = joined((local_top, local_total, picked_local), "vocab", combine_stats)
    loss = jnp.mean(top + jnp.log(total) - picked).reshape(1)
    grad_logits = (
        jnp.exp(logits - top[:, None]) / total[:, None] - hits.astype(jnp.float32)
    ).astype(jnp.bfloat16)
    d_weight = lax.dot_general(
        gathered, grad_logits, (((0,), (0,)), ((), ())), preferred_element_type=jnp.float32
    ).astype(jnp.bfloat16)
    own_rows = hidden.shape[0]
    partial_value = lax.dot_general(
        grad_logits, weight, (((1,), (1,)), ((), ())), preferred_element_type=jnp.float32
    )
    everything = lax.psum(partial_value, "vocab")
    summed = lax.dynamic_slice_in_dim(everything, lax.axis_index("vocab") * own_rows, own_rows, 0)
    return (loss, summed.astype(jnp.bfloat16), d_weight)


def solution(mesh):
    placed = (P(("dp", "vocab"), None), P(None, "vocab"), P("dp"))
    return jax.shard_map(
        body,
        mesh=mesh,
        in_specs=placed,
        out_specs=(P("dp"), P(("dp", "vocab"), None), P("dp", "vocab")),
        check_vma=False,
    )
```

profile of v0, /device:TPU:0, one launch (start us, length us, event | category | flops | bytes accessed | tf_op | source)
XLA Modules:
  0.0 96.6 jit_solution(8625070616558614490)
XLA Ops:
  0.6 0.0 copy-start
  0.6 1.2 %dynamic-slice = u32[1]{0:T(128)} dynamic-slice(u32[32]{0:T(128)} %constant.59, u32[]{:T(128)S(6)} %add.78), dynamic_slice_sizes={1} | dynamic-slice | bytes 12
  2.6 16.4 %all_gather.21 = bf16[64,3072]{1,0:T(8,128)(2,1)S(1)} all-gather(bf16[8,3072]{1,0:T(8,128)(2,1)} %param.5), channel_id=1, replica_groups=mesh['dp'=4,'vocab'=8] {'vocab'}, dimensions={0}, use_global_device_ids=true | all-gather | bytes 442368 | tf_op jit(solution)/shard_map/all_gather | solution.py:24
  19.0 4.1 %fusion.14 = (f32[64]{0:T(128)S(1)}, f32[64,1024]{1,0:T(8,128)S(1)}) fusion(bf16[64,3072]{1,0:T(8,128)(2,1)S(1)} %all_gather.21, bf16[3072,1024]{1,0:T(8,128)(2,1)} %param.6), kind=kOutput, calls=%fused_computation.21 | convolution fusion | flops 402718656 | bytes 6947072 | tf_op jit(solution)/shard_map/dot_general | solution.py:25
  23.1 0.2 dynamic-update-slice
  23.4 0.0 copy-done
  23.4 0.2 fusion.7
  23.6 0.2 dynamic-update-slice.2
  23.8 0.2 dynamic-update-slice.1
  24.0 17.2 %all-reduce.3 = (f32[512]{0:T(512)S(1)}, f32[512]{0:T(512)S(1)}, f32[512]{0:T(512)S(1)}) all-reduce(f32[512]{0:T(512)S(1)} %dynamic-update-slice, f32[512]{0:T(512)S(1)} %dynamic-update-slice.1, f32[512]{0:T(512)S(1)} %dynamic-update-slice.2), channel_id=2, replica_groups=mesh['dp'=4,'vocab'=8] {'vocab'}, use_global_device_ids=true, to_apply=%add | all-reduce | flops 1536 | bytes 12288
  41.2 0.1 reshape.21
  41.3 0.1 reshape.20
  41.4 0.1 reshape.19
  41.5 0.3 while.19
  41.8 0.6 subtract_reduce_fusion
  43.0 4.8 %fusion.11 = f32[64,3072]{1,0:T(8,128)S(1)} fusion(bf16[3072,1024]{1,0:T(8,128)(2,1)} %param.6, f32[64,1024]{1,0:T(8,128)S(1)} %get-tuple-element.210, f32[64]{0:T(128)S(1)} %get-tuple-element.182, f32[64]{0:T(128)S(1)} %get-tuple-element.181, s32[1024]{0:T(1024)S(1)} %iota_add_fusion, s32[64]{0:T(128)S(1)} %copy-done), kind=kOutput, calls=%fused_computation.20 | convolution fusion | flops 403046400 | bytes 7344896 | tf_op jit(solution)/shard_map/dot_general | solution.py:42
  47.9 33.8 %all-reduce.5 = bf16[64,3072]{1,0:T(8,128)(2,1)S(1)} all-reduce(f32[64,3072]{1,0:T(8,128)S(1)} %fusion.11), channel_id=1, replica_groups=mesh['dp'=4,'vocab'=8] {'vocab'}, use_global_device_ids=true, to_apply=%region_6.7 | all-reduce | flops 196608 | bytes 1179648 | tf_op jit(solution)/shard_map/psum | solution.py:45
  81.7 0.6 dynamic-slice_convert_fusion
  82.3 4.6 %convert_bitcast_fusion = bf16[3072,1024]{0,1:T(8,128)(2,1)} fusion(bf16[64,3072]{1,0:T(8,128)(2,1)S(1)} %all_gather.21, f32[64,1024]{1,0:T(8,128)S(1)} %get-tuple-element.210, f32[64]{0:T(128)S(1)} %get-tuple-element.182, f32[64]{0:T(128)S(1)} %get-tuple-element.181, s32[1024]{0:T(1024)S(1)} %iota_add_fusion, s32[64]{0:T(128)S(1)} %copy-done), kind=kOutput, calls=%fused_computation.10 | convolution fusion | flops 406192128 | bytes 6951680 | tf_op jit(solution)/shard_map/dot_general | solution.py:38
  86.9 8.6 %copy.6 = bf16[3072,1024]{1,0:T(8,128)(2,1)} copy(bf16[3072,1024]{0,1:T(8,128)(2,1)} %convert_bitcast_fusion) | data formatting | bytes 12582912
  (14 shorter events, 0.2 us)
Async XLA Ops:
  0.6 22.7 %copy-start = (s32[64]{0:T(128)S(1)}, s32[64]{0:T(128)}, u32[]{:S(2)}) copy-start(s32[64]{0:T(128)} %param.7) | copy-start | bytes 772
where the time goes:
time: 97.1 us; the launch traced here: 96.6 us
  blocking collectives  67.4 us (69%)
  matrix products  13.5 us (14%)
  local copies, waits for them, and re-layouts  11.4 us (12%)
  between operations  3.16 us (3%)
  other arithmetic  1.03 us (1%)
    psum x1, blocking collectives, body(): everything = lax.psum(partial_value, 'vocab')  33.8 us
    unnamed x1, blocking collectives  17.2 us
    all_gather x1, blocking collectives, body(): gathered = lax.all_gather(hidden, 'vocab', axis=0, tiled=True)  16.4 us
    unnamed x10, local copies, waits for them, and re-layouts  10.6 us
    dot_general x1, matrix products, body(): lax.dot_general(grad_logits, weight, (((1,), (1,)), ((), ())), preferred_...  4.85 us
    dot_general x1, matrix products, body(): lax.dot_general(gathered, grad_logits, (((0,), (0,)), ((), ())), preferre...  4.58 us
    dot_general x1, matrix products, body(): logits = jnp.dot(gathered, weight, preferred_element_type=jnp.float32)  4.09 us

commit v1 on v0

--- a/solution.py
+++ b/solution.py
@@ -42,7 +42,7 @@
     partial_value = lax.dot_general(
         grad_logits, weight, (((1,), (1,)), ((), ())), preferred_element_type=jnp.float32
     )
-    everything = lax.psum(partial_value, "vocab")
+    everything = jnp.sum(lax.all_gather(partial_value, "vocab"), 0)
     summed = lax.dynamic_slice_in_dim(everything, lax.axis_index("vocab") * own_rows, own_rows, 0)
     return (loss, summed.astype(jnp.bfloat16), d_weight)
 

time: 97.1 us -> 129 us (1.33)
  waiting for transfers between devices: 0 us -> 48.8 us
  blocking collectives: 67.4 us -> 33.6 us
  between operations: 3.16 us -> 16.5 us
  other arithmetic: 1.03 us -> 4.25 us
    all_gather x0 -> x1, waiting for transfers between devices: none -> 48.7 us  [body(): everything = jnp.sum(lax.all_gather(partial_value, 'vocab'), 0)]
    psum x1 -> x0, blocking collectives: 33.8 us -> none  [body(): everything = lax.psum(partial_value, 'vocab')]
    reduce_sum x0 -> x1, other arithmetic: none -> 3.22 us  [body(): everything = jnp.sum(lax.all_gather(partial_value, 'vocab'), 0)]
  transfers between devices with their start and end apart: 0 -> 1, of which waited for: 0 -> 1; matrix products, arithmetic and copies ran while one was open for 0% -> 11% of each run, Pallas kernels for 0% -> 0%
where the time goes in v1:
time: 129 us
  waiting for transfers between devices  48.8 us (38%)
  blocking collectives  33.6 us (26%)
  between operations  16.5 us (13%)
  matrix products  14.5 us (11%)
  local copies, waits for them, and re-layouts  11.3 us (9%)
  other arithmetic  4.25 us (3%)
    all_gather x1, waiting for transfers between devices, body(): everything = jnp.sum(lax.all_gather(partial_value, 'vocab'), 0)  48.7 us
    unnamed x1, blocking collectives  17.2 us
    all_gather x1, blocking collectives, body(): gathered = lax.all_gather(hidden, 'vocab', axis=0, tiled=True)  16.4 us
    unnamed x10, local copies, waits for them, and re-layouts  10.4 us
    dot_general x1, matrix products, body(): lax.dot_general(grad_logits, weight, (((1,), (1,)), ((), ())), preferred_...  5.78 us
    dot_general x1, matrix products, body(): lax.dot_general(gathered, grad_logits, (((0,), (0,)), ((), ())), preferre...  4.58 us
    dot_general x1, matrix products, body(): logits = jnp.dot(gathered, weight, preferred_element_type=jnp.float32)  4.09 us
    reduce_sum x1, other arithmetic, body(): everything = jnp.sum(lax.all_gather(partial_value, 'vocab'), 0)  3.22 us
  transfers between devices with their start and end apart: 1, of which 1 were waited for; matrix products, arithmetic and copies ran while one was open for 11% of the time, Pallas kernels for 0%

profile of v1, /device:TPU:0, one launch (start us, length us, event | category | flops | bytes accessed | tf_op | source)
XLA Modules:
  0.0 129.0 jit_solution(5680609029893360331)
XLA Ops:
  7.2 0.0 copy-start
  7.2 0.0 all-gather.6.cloned.1.call-start
  7.2 16.4 %all_gather.27 = bf16[64,3072]{1,0:T(8,128)(2,1)S(1)} all-gather(bf16[8,3072]{1,0:T(8,128)(2,1)} %param.5), channel_id=1, replica_groups=mesh['dp'=4,'vocab'=8] {'vocab'}, dimensions={0}, use_global_device_ids=true | all-gather | bytes 442368 | tf_op jit(solution)/shard_map/all_gather | solution.py:24
  23.7 1.2 dynamic-slice
  25.6 4.1 %fusion.14 = (f32[64]{0:T(128)S(1)}, f32[64,1024]{1,0:T(8,128)S(1)}) fusion(bf16[64,3072]{1,0:T(8,128)(2,1)S(1)} %all_gather.27, bf16[3072,1024]{1,0:T(8,128)(2,1)} %param.6), kind=kOutput, calls=%fused_computation.21 | convolution fusion | flops 402718656 | bytes 6947072 | tf_op jit(solution)/shard_map/dot_general | solution.py:25
  29.7 0.2 dynamic-update-slice
  29.9 0.0 copy-done
  29.9 0.2 fusion.7
  30.2 0.2 dynamic-update-slice.2
  30.4 0.2 dynamic-update-slice.1
  30.6 17.2 %all-reduce.3 = (f32[512]{0:T(512)S(1)}, f32[512]{0:T(512)S(1)}, f32[512]{0:T(512)S(1)}) all-reduce(f32[512]{0:T(512)S(1)} %dynamic-update-slice, f32[512]{0:T(512)S(1)} %dynamic-update-slice.1, f32[512]{0:T(512)S(1)} %dynamic-update-slice.2), channel_id=2, replica_groups=mesh['dp'=4,'vocab'=8] {'vocab'}, use_global_device_ids=true, to_apply=%add | all-reduce | flops 1536 | bytes 12288
  47.8 0.1 reshape.21
  47.9 0.1 reshape.20
  47.9 0.1 reshape.19
  48.0 0.3 while.19
  48.3 5.8 %fusion.11 = f32[64,3072]{1,0:T(8,128)} fusion(bf16[3072,1024]{1,0:T(8,128)(2,1)} %param.6, f32[64,1024]{1,0:T(8,128)S(1)} %get-tuple-element.210, f32[64]{0:T(128)S(1)} %get-tuple-element.182, f32[64]{0:T(128)S(1)} %get-tuple-element.181, s32[1024]{0:T(1024)S(1)} %iota_add_fusion, s32[64]{0:T(128)S(1)} %copy-done), kind=kOutput, calls=%fused_computation.20 | convolution fusion | flops 403046400 | bytes 7344896 | tf_op jit(solution)/shard_map/dot_general | solution.py:42
  54.1 0.0 all-gather.6.cloned.1.call-update
  54.1 4.6 %convert_bitcast_fusion = bf16[3072,1024]{0,1:T(8,128)(2,1)} fusion(bf16[64,3072]{1,0:T(8,128)(2,1)S(1)} %all_gather.27, f32[64,1024]{1,0:T(8,128)S(1)} %get-tuple-element.210, f32[64]{0:T(128)S(1)} %get-tuple-element.182, f32[64]{0:T(128)S(1)} %get-tuple-element.181, s32[1024]{0:T(1024)S(1)} %iota_add_fusion, s32[64]{0:T(128)S(1)} %copy-done), kind=kOutput, calls=%fused_computation.10 | convolution fusion | flops 406192128 | bytes 6951680 | tf_op jit(solution)/shard_map/dot_general | solution.py:38
  58.7 8.5 %copy.6 = bf16[3072,1024]{1,0:T(8,128)(2,1)} copy(bf16[3072,1024]{0,1:T(8,128)(2,1)} %convert_bitcast_fusion) | data formatting | bytes 12582912
  67.2 0.6 subtract_reduce_fusion
  68.4 48.7 %all-gather.6.cloned.1.call-done = f32[512,3072]{1,0:T(8,128)} async-done(((f32[64,3072]{1,0:T(8,128)}), f32[512,3072]{1,0:T(8,128)}) %all-gather.6.cloned.1.call-update) | async-done | bytes 6291472 | tf_op jit(solution)/shard_map/all_gather | solution.py:45
  117.2 3.2 %reduce_sum.39 = bf16[64,3072]{1,0:T(8,128)(2,1)S(1)} reduce(f32[8,64,3072]{2,1,0:T(8,128)} %bitcast.28, f32[]{:T(128)} %constant.50.clone.1), dimensions={0}, to_apply=%region_6.7 | reduce | flops 1376256 | bytes 6684676 | tf_op jit(solution)/shard_map/reduce_sum | solution.py:45
  120.4 0.6 dynamic-slice_convert_fusion
  (14 shorter events, 0.2 us)
Async XLA Ops:
  7.2 22.8 %copy-start = (s32[64]{0:T(128)S(1)}, s32[64]{0:T(128)}, u32[]{:S(2)}) copy-start(s32[64]{0:T(128)} %param.7) | copy-start | bytes 772
  7.2 110.0 %all-gather.6.cloned.1.call-start = ((), (), s32[]{:S(2)}) async-start(), calls=%async_computation | async-start | bytes 7077888 | tf_op jit(solution)/shard_map/all_gather | solution.py:45
Sparse Core Ops, SparseCore 0:
  54.2 62.8 all-gather.5
